TPU v7x, 256 devices: a whole 4x4x8 slice. The times are simulated.
256 devices in a mesh: wide: 64 (over x, y_hi, z), narrow: 4 (over y_lo, core).
Axes of the slice: x: 4, y: 4 (y_hi: 2, y_lo: 2; y = y_hi * 2 + y_lo), z: 8, core: 2. Of those that a mesh axis runs over, the one named last changes fastest.
Arguments:
- tokens: bfloat16 [8192, 2048], P('wide'), may hold values from -6 to 6
- expert_ids: int32 [8192, 6], P('wide'), may hold values from 0 to 63, all different within a row; in each aligned block of 128 rows (0 to 127, 128 to 255, ...) at most 16 rows name the same one
- gate_weights: float32 [8192, 6], P('wide'), may hold values from 0.05 to 0.6
- shared_gate: bfloat16 [2048, 2816], P('wide', 'narrow'), may hold values from -0.125 to 0.125
- shared_up: bfloat16 [2048, 2816], P('wide', 'narrow'), may hold values from -0.125 to 0.125
- shared_down: bfloat16 [2816, 2048], P('narrow', 'wide'), may hold values from -0.109375 to 0.109375
- expert_gate: bfloat16 [64, 2048, 1408], P('wide', None, 'narrow'), may hold values from -0.125 to 0.125
- expert_up: bfloat16 [64, 2048, 1408], P('wide', None, 'narrow'), may hold values from -0.125 to 0.125
- expert_down: bfloat16 [64, 1408, 2048], P('wide', 'narrow'), may hold values from -0.15625 to 0.15625
Outputs:
- moe_out: bfloat16 [8192, 2048], P('wide', 'narrow')
Inputs may be any that keep to these rules, and one draw needn't show every extreme that they name: `expert_ids`: the 6 ids of a row differ. Among the 128 rows of one index of wide, no expert is named by more than 16 rows.
All inputs are finite; a program needn't handle non-finite values.
Results may differ from a plain program's by a relative error of at most 0.0075.
Values may be sent and summed in bfloat16 or wider, within the bound.
No kernel may reach another device: no remote copies, remote signals or barrier semaphores. Data moves between devices by JAX's collectives and lax.ppermute only.
A program may use at most 128 MiB of HBM per device.

v0:
```python
import jax
import jax.numpy as jnp
from jax import lax
from jax.sharding import PartitionSpec as P


def items_in_groups(array, axis, split_dim, concat_dim, work, item_dim, out_dim):
    items = jax.tree.leaves(array)[0].shape[item_dim]
    count = 2 if items % 2 == 0 else 1
    finished = []
    for k in range(count):
        group = jax.tree.map(
            lambda a: lax.slice_in_dim(
                a, k * (items // count), (k + 1) * (items // count), axis=item_dim
            ),
            array,
        )
        finished.append(
            work(
                lax.all_to_all(
                    group, axis, split_axis=split_dim, concat_axis=concat_dim, tiled=True
                )
            )
        )
    return jax.tree.map(lambda *parts: jnp.concatenate(parts, axis=out_dim), *finished)


def split_up(array, dim, length):
    lengths = array.shape
    blocks = array.reshape(*lengths[:dim], length, lengths[dim] // length, *lengths[dim + 1 :])
    return jnp.moveaxis(blocks, dim, 0)


def sum_at_owner(array, axis, dim):
    length = lax.axis_size(axis)
    blocks = lax.all_to_all(split_up(array, dim, length), axis, 0, 0, tiled=True)
    return jnp.sum(blocks.astype(jnp.float32), axis=0)


def sent_together(arrays, axis, dim, along):
    ends, at = ([], 0)
    for a in arrays[:-1]:
        at += a.shape[along]
        ends.append(at)
    both = jnp.concatenate(arrays, axis=along)
    return tuple(jnp.split(lax.all_gather(both, axis, axis=dim, tiled=True), ends, axis=along))


def expert_ffn(received, w_gate, w_up, w_down):
    senders, items, width = received.shape
    flat_rows = received.reshape(senders * items, width)
    gate_part = jnp.dot(flat_rows, w_gate, preferred_element_type=jnp.float32)
    up_part = jnp.dot(flat_rows, w_up, preferred_element_type=jnp.float32)
    hidden = (jax.nn.silu(gate_part) * up_part).astype(jnp.bfloat16)
    partial_value = jnp.dot(hidden, w_down, preferred_element_type=jnp.float32).astype(jnp.bfloat16)
    return partial_value.reshape(senders, items, w_down.shape[1])


def body(
    tokens,
    expert_ids,
    gate_weights,
    shared_gate,
    shared_up,
    shared_down,
    expert_gate,
    expert_up,
    expert_down,
):
    tok_count, width = tokens.shape
    top_count = expert_ids.shape[1]
    experts = lax.axis_size("wide") * expert_gate.shape[0]
    capacity = min(tok_count, 4 * tok_count * top_count // (3 * experts))
    w_gate = expert_gate[0]
    w_up = expert_up[0]
    w_down = expert_down[0]
    pairs = tok_count * top_count
    flat_ids = expert_ids.reshape(pairs)
    onehot = (flat_ids[:, None] == jnp.arange(experts, dtype=jnp.int32)[None, :]).astype(jnp.int32)
    before = jnp.cumsum(onehot, axis=0) - onehot
    slot_pos = jnp.sum(before * onehot, axis=1)
    target_slot = flat_ids * capacity + slot_pos
    source = (
        jnp.full((experts * capacity,), -1, jnp.int32)
        .at[target_slot]
        .set(jnp.arange(pairs, dtype=jnp.int32))
    )
    filled = source >= 0
    token_of = jnp.where(filled, source // top_count, 0)
    outgoing = jnp.where(filled[:, None], tokens[token_of], jnp.zeros((), jnp.bfloat16))
    outgoing = outgoing.reshape(experts, capacity, width)

    def run_expert(received):
        return expert_ffn(received, w_gate, w_up, w_down)

    partial_value = items_in_groups(outgoing, "wide", 0, 0, run_expert, 1, 1)
    expert_out = sum_at_owner(partial_value, "narrow", 2).astype(jnp.bfloat16)
    returned = lax.all_to_all(expert_out, "wide", split_axis=0, concat_axis=0, tiled=True)
    returned_rows = returned.reshape(experts * capacity, returned.shape[2])
    pair_rows = returned_rows[target_slot].astype(jnp.float32)
    weighted = gate_weights.reshape(pairs, 1) * pair_rows
    routed = jnp.sum(weighted.reshape(tok_count, top_count, returned.shape[2]), axis=1)
    blocks = sent_together((shared_gate, shared_up), "wide", 0, 1)
    gate_sum = jnp.dot(tokens, blocks[0], preferred_element_type=jnp.float32)
    up_sum = jnp.dot(tokens, blocks[1], preferred_element_type=jnp.float32)
    shared_hidden = (jax.nn.silu(gate_sum) * up_sum).astype(jnp.bfloat16)
    shared_terms = jnp.dot(
        shared_hidden,
        lax.all_gather(shared_down, "wide", axis=1, tiled=True),
        preferred_element_type=jnp.float32,
    )
    shared = sum_at_owner(shared_terms.astype(jnp.bfloat16), "narrow", 1)
    return (shared + routed).astype(jnp.bfloat16)


def solution(mesh):
    in_specs = (
        P("wide", None),
        P("wide", None),
        P("wide", None),
        P("wide", "narrow"),
        P("wide", "narrow"),
        P("narrow", "wide"),
        P("wide", None, "narrow"),
        P("wide", None, "narrow"),
        P("wide", "narrow", None),
    )
    out_specs = P("wide", "narrow")
    return jax.shard_map(body, mesh=mesh, in_specs=in_specs, out_specs=out_specs, check_vma=False)
```

profile of v0, /device:TPU:1, one launch (start us, length us, event | category | flops | bytes accessed | tf_op | source)
XLA Modules:
  0.0 334.1 jit_solution(4834467579335310039)
XLA Ops:
  6.5 1.7 pad_maximum_fusion.1
  8.3 0.8 copy.19
  9.3 0.7 broadcast_multiply_fusion
  10.3 1.8 reduce-window.6
  12.6 3.4 %scatter_custom_fusion = s32[1024]{0:T(1024)S(1)} fusion(s32[768]{0:T(1024)S(1)} %fusion.85, s32[768]{0:T(1024)S(1)} %iota.11, s32[]{:T(128)} %constant.16.clone.1), kind=kCustom, calls=%fused_computation.79 | custom fusion | bytes 4100 | tf_op jit(solution)/shard_map/scatter | solution.py:86
  16.1 6.1 %gather_fusion = bf16[1024,2048]{1,0:T(8,128)(2,1)} fusion(bf16[128,2048]{1,0:T(8,128)(2,1)S(1)} %copy-done.1, s32[1024]{0:T(1024)S(1)} %fusion.83), kind=kCustom, calls=%fused_computation | custom fusion | bytes 8392704 | tf_op jit(solution)/shard_map/gather | solution.py:90
  22.2 2.5 broadcast_select_fusion
  24.7 1.8 fusion.91
  26.5 68.2 %all_to_all.25 = bf16[64,8,2048]{2,1,0:T(8,128)(2,1)} all-to-all(bf16[64,8,2048]{2,1,0:T(8,128)(2,1)S(1)} %get-tuple-element.6), channel_id=1, replica_groups=mesh['wide'=64,'narrow'=4] {'wide'}, dimensions={0} | all-to-all | bytes 4194304 | tf_op jit(solution)/shard_map/all_to_all | solution.py:20
  94.7 10.2 %all-to-all-start.1 = ((bf16[64,8,2048]{2,1,0:T(8,128)(2,1)}), bf16[64,8,2048]{2,1,0:T(8,128)(2,1)}, u32[]{:S(2)}, u32[]{:S(2)}) async-start(bf16[64,8,2048]{2,1,0:T(8,128)(2,1)} %get-tuple-element.5), calls=%async_computation.1 | async-start | bytes 4194304 | tf_op jit(solution)/shard_map/all_to_all | solution.py:20
  105.0 0.7 all-gather.5.cloned.1.call-update
  105.7 3.4 %fusion.6 = f32[512,352]{0,1:T(8,128)} fusion(bf16[64,8,2048]{2,1,0:T(8,128)(2,1)} %all_to_all.25, bf16[1,2048,352]{1,2,0:T(8,128)(2,1)S(1)} %copy-done.3), kind=kOutput, calls=%fused_computation.15 | convolution fusion | flops 738197504 | bytes 4259840 | tf_op jit(solution)/shard_map/dot_general | solution.py:52
  109.1 5.7 %convolution_convert_fusion = bf16[512,2048]{1,0:T(8,128)(2,1)} fusion(bf16[1,352,2048]{2,1,0:T(8,128)(2,1)S(1)} %copy-done, bf16[1,2048,352]{1,2,0:T(8,128)(2,1)} %param.16, bf16[64,8,2048]{2,1,0:T(8,128)(2,1)} %all_to_all.25, f32[512,352]{0,1:T(8,128)} %fusion.6), kind=kOutput, calls=%fused_computation.10 | convolution fusion | flops 1478524928 | bytes 7798784 | tf_op jit(solution)/shard_map/dot_general | solution.py:55
  114.8 46.5 %all-to-all-done.1 = bf16[64,8,2048]{2,1,0:T(8,128)(2,1)} async-done(((bf16[64,8,2048]{2,1,0:T(8,128)(2,1)}), bf16[64,8,2048]{2,1,0:T(8,128)(2,1)}, u32[]{:S(2)}, u32[]{:S(2)}) %all-to-all-start.1) | async-done | bytes 2097184 | tf_op jit(solution)/shard_map/all_to_all | solution.py:20
  161.3 3.4 %fusion.10 = f32[512,352]{0,1:T(8,128)} fusion(bf16[64,8,2048]{2,1,0:T(8,128)(2,1)} %all-to-all-done.1, bf16[1,2048,352]{1,2,0:T(8,128)(2,1)S(1)} %copy-done.3), kind=kOutput, calls=%fused_computation.19 | convolution fusion | flops 738197504 | bytes 4259840 | tf_op jit(solution)/shard_map/dot_general | solution.py:52
  164.7 5.8 %convolution_convert_fusion.1 = bf16[512,2048]{1,0:T(8,128)(2,1)} fusion(bf16[1,352,2048]{2,1,0:T(8,128)(2,1)S(1)} %copy-done, bf16[1,2048,352]{1,2,0:T(8,128)(2,1)} %param.16, bf16[64,8,2048]{2,1,0:T(8,128)(2,1)} %all-to-all-done.1, f32[512,352]{0,1:T(8,128)} %fusion.10), kind=kOutput, calls=%fused_computation.11 | convolution fusion | flops 1478524928 | bytes 7798784 | tf_op jit(solution)/shard_map/dot_general | solution.py:55
  170.5 2.5 copy_bitcast_fusion
  173.0 59.4 %all_to_all.26 = bf16[4,64,16,512]{3,2,1,0:T(8,128)(2,1)} all-to-all(bf16[4,64,16,512]{3,2,1,0:T(8,128)(2,1)S(1)} %copy_bitcast_fusion), channel_id=1, replica_groups=mesh['wide'=64,'narrow'=4] {'narrow'}, dimensions={0} | all-to-all | bytes 8388608 | tf_op jit(solution)/shard_map/all_to_all | solution.py:36
  232.4 4.4 %reduce_sum.44 = bf16[64,16,512]{2,1,0:T(8,128)(2,1)} reduce(bf16[4,64,16,512]{3,2,1,0:T(8,128)(2,1)} %all_to_all.26, bf16[]{:T(256)} %constant.35.clone.1), dimensions={0}, to_apply=%region_5.6 | reduce | flops 1572864 | bytes 5242882 | tf_op jit(solution)/shard_map/reduce_sum | solution.py:37
  236.9 9.4 %all-to-all-start.4 = ((bf16[64,16,512]{2,1,0:T(8,128)(2,1)}), bf16[64,16,512]{2,1,0:T(8,128)(2,1)S(1)}, u32[]{:S(2)}, u32[]{:S(2)}) async-start(bf16[64,16,512]{2,1,0:T(8,128)(2,1)} %reduce_sum.44), calls=%async_computation.4 | async-start | bytes 2097152 | tf_op jit(solution)/shard_map/all_to_all | solution.py:98
  246.3 3.6 %fusion.38 = f32[128,704]{0,1:T(8,128)} fusion(bf16[128,2048]{1,0:T(8,128)(2,1)S(1)} %copy-done.1, bf16[2048,1408]{1,0:T(8,128)(2,1)} %all-gather.3.cloned.1.call-done), kind=kOutput, calls=%fused_computation.32 | convolution fusion | flops 369098752 | bytes 4030464 | tf_op jit(solution)/shard_map/dot_general | solution.py:104
  250.0 50.0 %all-gather.5.cloned.1.call-done = bf16[704,2048]{0,1:T(8,128)(2,1)} async-done(((bf16[704,32]{0,1:T(8,128)(2,1)}), bf16[704,2048]{0,1:T(8,128)(2,1)}) %all-gather.5.cloned.1.call-update) | async-done | bytes 2883600 | tf_op jit(solution)/shard_map/all_gather | solution.py:109
  299.9 7.4 %convolution_convert_fusion.2 = bf16[128,2048]{1,0:T(8,128)(2,1)S(1)} fusion(bf16[704,2048]{0,1:T(8,128)(2,1)} %all-gather.5.cloned.1.call-done, bf16[128,2048]{1,0:T(8,128)(2,1)S(1)} %copy-done.1, bf16[2048,1408]{1,0:T(8,128)(2,1)} %all-gather.3.cloned.1.call-done, f32[128,704]{0,1:T(8,128)} %fusion.38), kind=kOutput, calls=%fused_computation.12 | convolution fusion | flops 739000320 | bytes 7700480 | tf_op jit(solution)/shard_map/dot_general | solution.py:107
  307.3 0.8 copy.30
  308.2 8.4 %all-to-all-start = ((bf16[4,128,512]{2,1,0:T(8,128)(2,1)}), bf16[4,128,512]{2,1,0:T(8,128)(2,1)}, u32[]{:S(2)}, u32[]{:S(2)}) async-start(bf16[4,128,512]{2,1,0:T(8,128)(2,1)} %bitcast.93), calls=%async_computation | async-start | bytes 1048576 | tf_op jit(solution)/shard_map/all_to_all | solution.py:36
  316.6 0.7 copy.17
  317.3 3.3 gather_fusion.1
  320.6 1.3 reshape.89
  321.9 2.2 multiply_reduce_fusion
  324.1 0.4 all-to-all-done
  324.5 1.1 convert_reduce_fusion
  325.7 1.6 add_convert_fusion
  (27 shorter events, 1.2 us)
Async XLA Ops:
  6.5 102.6 %copy-start = (bf16[1,352,2048]{2,1,0:T(8,128)(2,1)S(1)}, bf16[1,352,2048]{2,1,0:T(8,128)(2,1)}, u32[]{:S(2)}) copy-start(bf16[1,352,2048]{2,1,0:T(8,128)(2,1)} %param.17) | copy-start | bytes 4325380
  6.5 9.6 %copy-start.1 = (bf16[128,2048]{1,0:T(8,128)(2,1)S(1)}, bf16[128,2048]{1,0:T(8,128)(2,1)}, u32[]{:S(2)}) copy-start(bf16[128,2048]{1,0:T(8,128)(2,1)} %param.9) | copy-start | bytes 1572868
  6.5 239.8 %all-gather.3.cloned.1.call-start = ((), (), s32[]{:S(2)}) async-start(), calls=%async_computation.5 | async-start | bytes 5857280 | tf_op jit(solution)/shard_map/all_gather | solution.py:46
  94.7 11.0 %copy-start.3 = (bf16[1,2048,352]{1,2,0:T(8,128)(2,1)S(1)}, bf16[1,2048,352]{1,2,0:T(8,128)(2,1)}, u32[]{:S(2)}) copy-start(bf16[1,2048,352]{1,2,0:T(8,128)(2,1)} %param.15) | copy-start | bytes 4325380
  94.7 66.6 %all-to-all-start.1 = ((bf16[64,8,2048]{2,1,0:T(8,128)(2,1)}), bf16[64,8,2048]{2,1,0:T(8,128)(2,1)}, u32[]{:S(2)}, u32[]{:S(2)}) async-start(bf16[64,8,2048]{2,1,0:T(8,128)(2,1)} %get-tuple-element.5), calls=%async_computation.1 | async-start | bytes 4194304 | tf_op jit(solution)/shard_map/all_to_all | solution.py:20
  104.9 195.0 %all-gather.5.cloned.1.call-start = ((), (), s32[]{:S(2)}) async-start(), calls=%async_computation.6 | async-start | bytes 3194880 | tf_op jit(solution)/shard_map/all_gather | solution.py:109
  236.9 71.3 %all-to-all-start.4 = ((bf16[64,16,512]{2,1,0:T(8,128)(2,1)}), bf16[64,16,512]{2,1,0:T(8,128)(2,1)S(1)}, u32[]{:S(2)}, u32[]{:S(2)}) async-start(bf16[64,16,512]{2,1,0:T(8,128)(2,1)} %reduce_sum.44), calls=%async_computation.4 | async-start | bytes 2097152 | tf_op jit(solution)/shard_map/all_to_all | solution.py:98
  307.3 9.2 %copy-start.2 = (f32[128,6]{0,1:T(8,128)S(1)}, f32[128,6]{0,1:T(8,128)}, u32[]{:S(2)}) copy-start(f32[128,6]{0,1:T(8,128)} %param.11) | copy-start | bytes 9220
  308.2 16.3 %all-to-all-start = ((bf16[4,128,512]{2,1,0:T(8,128)(2,1)}), bf16[4,128,512]{2,1,0:T(8,128)(2,1)}, u32[]{:S(2)}, u32[]{:S(2)}) async-start(bf16[4,128,512]{2,1,0:T(8,128)(2,1)} %bitcast.93), calls=%async_computation | async-start | bytes 1048576 | tf_op jit(solution)/shard_map/all_to_all | solution.py:36
Sparse Core Ops, SparseCore 0:
  10.8 162.8 all-gather.2
  177.4 122.4 all-gather.4
where the time goes:
time: 335 us; the launch traced here: 334 us
  blocking collectives  128 us (38%)
  waiting for transfers between devices  97.5 us (29%)
  matrix products  29.3 us (9%)
  starting transfers between devices  28.1 us (8%)
  local copies, waits for them, and re-layouts  19.1 us (6%)
  other arithmetic  18.9 us (6%)
  between operations  13.6 us (4%)
    all_to_all x1, blocking collectives, items_in_groups(): lax.all_to_all(group, axis, split_axis=split_dim, concat_axis=concat_dim,...  68.2 us
    all_to_all x1, blocking collectives, sum_at_owner(): lax.all_to_all(split_up(array, dim, length), axis, 0, 0, tiled=True)  59.4 us
    all_gather x1, waiting for transfers between devices, body(): lax.all_gather(shared_down, 'wide', axis=1, tiled=True)  50 us
    all_to_all x1, waiting for transfers between devices, items_in_groups(): lax.all_to_all(group, axis, split_axis=split_dim, concat_axis=concat_dim,...  46.5 us
    dot_general x2, matrix products, expert_ffn(): jnp.dot(hidden, w_down, preferred_element_type=jnp.float32)  11.5 us
    all_to_all x1, starting transfers between devices, items_in_groups(): lax.all_to_all(group, axis, split_axis=split_dim, concat_axis=concat_dim,...  10.2 us
    all_to_all x1, starting transfers between devices, body(): lax.all_to_all(expert_out, 'wide', split_axis=0, concat_axis=0, tiled=True)  9.44 us
    all_to_all x1, starting transfers between devices, sum_at_owner(): lax.all_to_all(split_up(array, dim, length), axis, 0, 0, tiled=True)  8.38 us
  transfers between devices with their start and end apart: 5, of which 3 were waited for; matrix products, arithmetic and copies ran while one was open for 19% of the time, Pallas kernels for 0%

commit v1 on v0

--- a/solution.py
+++ b/solution.py
@@ -2,6 +2,11 @@
 import jax.numpy as jnp
 from jax import lax
 from jax.sharding import PartitionSpec as P
+
+
+def gather_over(block, name, along):
+    outgoing = jnp.stack([block] * lax.axis_size(name))
+    return jnp.concatenate(lax.all_to_all(outgoing, name, 0, 0), axis=along)
 
 
 def items_in_groups(array, axis, split_dim, concat_dim, work, item_dim, out_dim):
@@ -105,9 +110,7 @@
     up_sum = jnp.dot(tokens, blocks[1], preferred_element_type=jnp.float32)
     shared_hidden = (jax.nn.silu(gate_sum) * up_sum).astype(jnp.bfloat16)
     shared_terms = jnp.dot(
-        shared_hidden,
-        lax.all_gather(shared_down, "wide", axis=1, tiled=True),
-        preferred_element_type=jnp.float32,
+        shared_hidden, gather_over(shared_down, "wide", 1), preferred_element_type=jnp.float32
     )
     shared = sum_at_owner(shared_terms.astype(jnp.bfloat16), "narrow", 1)
     return (shared + routed).astype(jnp.bfloat16)

time: 335 us -> 387 us (1.16)
  waiting for transfers between devices: 97.5 us -> 133 us
  blocking collectives: 128 us -> 141 us
    all_to_all x0 -> x1, waiting for transfers between devices: none -> 72.5 us  [gather_over(): return jnp.concatenate(lax.all_to_all(outgoing, name, 0, 0), axis=along)]
    all_gather x1 -> x0, waiting for transfers between devices: 50 us -> none  [body(): lax.all_gather(shared_down, 'wide', axis=1, tiled=True)]
    all_to_all x1, blocking collectives: 59.4 us -> 76.9 us  [sum_at_owner(): lax.all_to_all(split_up(array, dim, length), axis, 0, 0, tiled=True)]
    all_to_all x1, waiting for transfers between devices: 0.01 us -> 14.9 us  [body(): lax.all_to_all(expert_out, 'wide', split_axis=0, concat_axis=0, tiled=True)]
    all_to_all x0 -> x1, starting transfers between devices: none -> 6.18 us  [gather_over(): return jnp.concatenate(lax.all_to_all(outgoing, name, 0, 0), axis=along)]
    all_to_all x1, blocking collectives: 68.2 us -> 64 us  [items_in_groups(): lax.all_to_all(group, axis, split_axis=split_dim, concat_axis=concat_dim,...]
  transfers between devices with their start and end apart: 5 -> 5, of which waited for: 3 -> 3; matrix products, arithmetic and copies ran while one was open for 19% -> 12% of each run, Pallas kernels for 0% -> 0%
where the time goes in v1:
time: 387 us; the launch traced here: 386 us
  blocking collectives  141 us (36%)
  waiting for transfers between devices  133 us (34%)
  starting transfers between devices  31.5 us (8%)
  matrix products  29 us (7%)
  local copies, waits for them, and re-layouts  21.6 us (6%)
  other arithmetic  16.2 us (4%)
  between operations  13.6 us (4%)
    all_to_all x1, blocking collectives, sum_at_owner(): lax.all_to_all(split_up(array, dim, length), axis, 0, 0, tiled=True)  76.9 us
    all_to_all x1, waiting for transfers between devices, gather_over(): return jnp.concatenate(lax.all_to_all(outgoing, name, 0, 0), axis=along)  72.5 us
    all_to_all x1, blocking collectives, items_in_groups(): lax.all_to_all(group, axis, split_axis=split_dim, concat_axis=concat_dim,...  64 us
    all_to_all x1, waiting for transfers between devices, items_in_groups(): lax.all_to_all(group, axis, split_axis=split_dim, concat_axis=concat_dim,...  45.9 us
    all_to_all x1, waiting for transfers between devices, body(): lax.all_to_all(expert_out, 'wide', split_axis=0, concat_axis=0, tiled=True)  14.9 us
    dot_general x2, matrix products, expert_ffn(): jnp.dot(hidden, w_down, preferred_element_type=jnp.float32)  11.1 us
    all_to_all x1, starting transfers between devices, items_in_groups(): lax.all_to_all(group, axis, split_axis=split_dim, concat_axis=concat_dim,...  9.59 us
    all_to_all x1, starting transfers between devices, sum_at_owner(): lax.all_to_all(split_up(array, dim, length), axis, 0, 0, tiled=True)  8.03 us
  transfers between devices with their start and end apart: 5, of which 3 were waited for; matrix products, arithmetic and copies ran while one was open for 12% of the time, Pallas kernels for 0%

profile of v1, /device:TPU:1, one launch (start us, length us, event | category | flops | bytes accessed | tf_op | source)
XLA Modules:
  0.0 386.3 jit_solution(1035290873174867259)
XLA Ops:
  6.5 0.8 broadcast_multiply_fusion
  7.4 0.8 copy.20
  8.7 1.8 reduce-window.6
  10.5 0.3 slice_reduce_fusion
  11.0 3.4 scatter_custom_fusion
  14.5 6.0 %gather_fusion = bf16[1024,2048]{1,0:T(8,128)(2,1)} fusion(bf16[128,2048]{1,0:T(8,128)(2,1)S(1)} %copy-done.1, s32[1024]{0:T(1024)S(1)} %fusion.83), kind=kCustom, calls=%fused_computation | custom fusion | bytes 8392704 | tf_op jit(solution)/shard_map/gather | solution.py:95
  20.5 2.5 broadcast_select_fusion
  23.1 1.7 fusion.91
  24.8 64.0 %all_to_all.30 = bf16[64,8,2048]{2,1,0:T(8,128)(2,1)} all-to-all(bf16[64,8,2048]{2,1,0:T(8,128)(2,1)S(1)} %get-tuple-element.6), channel_id=1, replica_groups=mesh['wide'=64,'narrow'=4] {'wide'}, dimensions={0} | all-to-all | bytes 4194304 | tf_op jit(solution)/shard_map/all_to_all | solution.py:25
  88.8 9.6 %all-to-all-start.2 = ((bf16[64,8,2048]{2,1,0:T(8,128)(2,1)}), bf16[64,8,2048]{2,1,0:T(8,128)(2,1)}, u32[]{:S(2)}, u32[]{:S(2)}) async-start(bf16[64,8,2048]{2,1,0:T(8,128)(2,1)} %get-tuple-element.5), calls=%async_computation.2 | async-start | bytes 4194304 | tf_op jit(solution)/shard_map/all_to_all | solution.py:25
  98.5 0.7 pad_maximum_fusion.1
  99.2 3.5 fusion.6
  102.7 45.9 %all-to-all-done.2 = bf16[64,8,2048]{2,1,0:T(8,128)(2,1)} async-done(((bf16[64,8,2048]{2,1,0:T(8,128)(2,1)}), bf16[64,8,2048]{2,1,0:T(8,128)(2,1)}, u32[]{:S(2)}, u32[]{:S(2)}) %all-to-all-start.2) | async-done | bytes 2097184 | tf_op jit(solution)/shard_map/all_to_all | solution.py:25
  148.5 3.4 fusion.10
  151.9 5.8 %convolution_convert_fusion = bf16[512,2048]{1,0:T(8,128)(2,1)} fusion(bf16[1,352,2048]{2,1,0:T(8,128)(2,1)S(1)} %copy-done, bf16[1,2048,352]{1,2,0:T(8,128)(2,1)} %param.16, bf16[64,8,2048]{2,1,0:T(8,128)(2,1)} %all_to_all.30, f32[512,352]{0,1:T(8,128)} %fusion.6), kind=kOutput, calls=%fused_computation.10 | convolution fusion | flops 1478524928 | bytes 7798784 | tf_op jit(solution)/shard_map/dot_general | solution.py:60
  157.7 5.3 %convolution_convert_fusion.1 = bf16[512,2048]{1,0:T(8,128)(2,1)} fusion(bf16[1,352,2048]{2,1,0:T(8,128)(2,1)S(1)} %copy-done, bf16[1,2048,352]{1,2,0:T(8,128)(2,1)S(1)} %copy-done.7, bf16[64,8,2048]{2,1,0:T(8,128)(2,1)} %all-to-all-done.2, f32[512,352]{0,1:T(8,128)} %fusion.10), kind=kOutput, calls=%fused_computation.11 | convolution fusion | flops 1478524928 | bytes 7798784 | tf_op jit(solution)/shard_map/dot_general | solution.py:60
  163.1 2.5 copy_bitcast_fusion
  165.6 76.9 %all_to_all.31 = bf16[4,64,16,512]{3,2,1,0:T(8,128)(2,1)} all-to-all(bf16[4,64,16,512]{3,2,1,0:T(8,128)(2,1)S(1)} %copy_bitcast_fusion), channel_id=1, replica_groups=mesh['wide'=64,'narrow'=4] {'narrow'}, dimensions={0} | all-to-all | bytes 8388608 | tf_op jit(solution)/shard_map/all_to_all | solution.py:41
  242.6 2.0 stack.2
  244.6 6.2 %all-to-all-start = ((bf16[64,704,32]{1,2,0:T(8,128)(2,1)}), bf16[64,704,32]{1,2,0:T(8,128)(2,1)}, u32[]{:S(2)}, u32[]{:S(2)}) async-start(bf16[64,704,32]{1,2,0:T(8,128)(2,1)} %stack.2), calls=%async_computation | async-start | bytes 6291456 | tf_op jit(solution)/shard_map/all_to_all | solution.py:9
  250.8 4.4 %reduce_sum.44 = bf16[64,16,512]{2,1,0:T(8,128)(2,1)} reduce(bf16[4,64,16,512]{3,2,1,0:T(8,128)(2,1)} %all_to_all.31, bf16[]{:T(256)} %constant.35.clone.1), dimensions={0}, to_apply=%region_5.6 | reduce | flops 1572864 | bytes 5242882 | tf_op jit(solution)/shard_map/reduce_sum | solution.py:42
  255.2 72.5 %all-to-all-done = bf16[64,704,32]{1,2,0:T(8,128)(2,1)} async-done(((bf16[64,704,32]{1,2,0:T(8,128)(2,1)}), bf16[64,704,32]{1,2,0:T(8,128)(2,1)}, u32[]{:S(2)}, u32[]{:S(2)}) %all-to-all-start) | async-done | bytes 2883616 | tf_op jit(solution)/shard_map/all_to_all | solution.py:9
  327.7 7.7 %all-to-all-start.5 = ((bf16[64,16,512]{2,1,0:T(8,128)(2,1)}), bf16[64,16,512]{2,1,0:T(8,128)(2,1)S(1)}, u32[]{:S(2)}, u32[]{:S(2)}) async-start(bf16[64,16,512]{2,1,0:T(8,128)(2,1)} %reduce_sum.44), calls=%async_computation.5 | async-start | bytes 2097152 | tf_op jit(solution)/shard_map/all_to_all | solution.py:103
  335.5 3.7 fusion.38
  339.1 7.4 %convolution_convert_fusion.2 = bf16[128,2048]{1,0:T(8,128)(2,1)S(1)} fusion(bf16[704,2048]{0,1:T(8,128)(2,1)} %bitcast.3, bf16[128,2048]{1,0:T(8,128)(2,1)S(1)} %copy-done.1, bf16[2048,1408]{1,0:T(8,128)(2,1)} %all-gather.2.cloned.1.call-done, f32[128,704]{0,1:T(8,128)} %fusion.38), kind=kOutput, calls=%fused_computation.12 | convolution fusion | flops 739000320 | bytes 7700480 | tf_op jit(solution)/shard_map/dot_general | solution.py:112
  346.5 0.9 copy.31
  347.4 14.9 %all-to-all-done.5 = bf16[64,16,512]{2,1,0:T(8,128)(2,1)S(1)} async-done(((bf16[64,16,512]{2,1,0:T(8,128)(2,1)}), bf16[64,16,512]{2,1,0:T(8,128)(2,1)S(1)}, u32[]{:S(2)}, u32[]{:S(2)}) %all-to-all-start.5) | async-done | bytes 1048608 | tf_op jit(solution)/shard_map/all_to_all | solution.py:103
  362.3 8.0 %all-to-all-start.1 = ((bf16[4,128,512]{2,1,0:T(8,128)(2,1)}), bf16[4,128,512]{2,1,0:T(8,128)(2,1)S(1)}, u32[]{:S(2)}, u32[]{:S(2)}) async-start(bf16[4,128,512]{2,1,0:T(8,128)(2,1)} %bitcast.96), calls=%async_computation.1 | async-start | bytes 1048576 | tf_op jit(solution)/shard_map/all_to_all | solution.py:41
  370.5 3.3 gather_fusion.1
  373.8 2.5 reshape.99
  376.3 2.3 multiply_reduce_fusion
  378.7 0.7 add_convert_fusion
  (35 shorter events, 1.1 us)
Async XLA Ops:
  6.5 145.4 %copy-start = (bf16[1,352,2048]{2,1,0:T(8,128)(2,1)S(1)}, bf16[1,352,2048]{2,1,0:T(8,128)(2,1)}, u32[]{:S(2)}) copy-start(bf16[1,352,2048]{2,1,0:T(8,128)(2,1)} %param.17) | copy-start | bytes 4325380
  6.5 8.0 %copy-start.1 = (bf16[128,2048]{1,0:T(8,128)(2,1)S(1)}, bf16[128,2048]{1,0:T(8,128)(2,1)}, u32[]{:S(2)}) copy-start(bf16[128,2048]{1,0:T(8,128)(2,1)} %param.9) | copy-start | bytes 1572868
  88.8 9.7 %copy-start.2 = (bf16[32,704]{1,0:T(8,128)(2,1)S(1)}, bf16[32,704]{1,0:T(8,128)(2,1)}, u32[]{:S(2)}) copy-start(bf16[32,704]{1,0:T(8,128)(2,1)} %param.13) | copy-start | bytes 135172
  88.8 9.7 %copy-start.3 = (bf16[32,704]{1,0:T(8,128)(2,1)S(1)}, bf16[32,704]{1,0:T(8,128)(2,1)}, u32[]{:S(2)}) copy-start(bf16[32,704]{1,0:T(8,128)(2,1)} %param.12) | copy-start | bytes 135172
  88.8 10.4 %copy-start.6 = (bf16[1,2048,352]{1,2,0:T(8,128)(2,1)S(1)}, bf16[1,2048,352]{1,2,0:T(8,128)(2,1)}, u32[]{:S(2)}) copy-start(bf16[1,2048,352]{1,2,0:T(8,128)(2,1)} %param.15) | copy-start | bytes 4325380
  88.8 59.7 %all-to-all-start.2 = ((bf16[64,8,2048]{2,1,0:T(8,128)(2,1)}), bf16[64,8,2048]{2,1,0:T(8,128)(2,1)}, u32[]{:S(2)}, u32[]{:S(2)}) async-start(bf16[64,8,2048]{2,1,0:T(8,128)(2,1)} %get-tuple-element.5), calls=%async_computation.2 | async-start | bytes 4194304 | tf_op jit(solution)/shard_map/all_to_all | solution.py:25
  98.4 237.1 %all-gather.2.cloned.1.call-start = ((), (), s32[]{:S(2)}) async-start(), calls=%async_computation.6 | async-start | bytes 5857280 | tf_op jit(solution)/shard_map/all_gather | solution.py:51
  151.9 5.8 %copy-start.7 = (bf16[1,2048,352]{1,2,0:T(8,128)(2,1)S(1)}, bf16[1,2048,352]{1,2,0:T(8,128)(2,1)}, u32[]{:S(2)}) copy-start(bf16[1,2048,352]{1,2,0:T(8,128)(2,1)} %param.16) | copy-start | bytes 4325380
  165.6 77.0 %copy-start.4 = (bf16[704,32]{0,1:T(8,128)(2,1)S(1)}, bf16[704,32]{0,1:T(8,128)(2,1)}, u32[]{:S(2)}) copy-start(bf16[704,32]{0,1:T(8,128)(2,1)} %param.14) | copy-start | bytes 135172
  244.6 83.1 %all-to-all-start = ((bf16[64,704,32]{1,2,0:T(8,128)(2,1)}), bf16[64,704,32]{1,2,0:T(8,128)(2,1)}, u32[]{:S(2)}, u32[]{:S(2)}) async-start(bf16[64,704,32]{1,2,0:T(8,128)(2,1)} %stack.2), calls=%async_computation | async-start | bytes 6291456 | tf_op jit(solution)/shard_map/all_to_all | solution.py:9
  327.7 34.6 %all-to-all-start.5 = ((bf16[64,16,512]{2,1,0:T(8,128)(2,1)}), bf16[64,16,512]{2,1,0:T(8,128)(2,1)S(1)}, u32[]{:S(2)}, u32[]{:S(2)}) async-start(bf16[64,16,512]{2,1,0:T(8,128)(2,1)} %reduce_sum.44), calls=%async_computation.5 | async-start | bytes 2097152 | tf_op jit(solution)/shard_map/all_to_all | solution.py:103
  346.5 23.8 %copy-start.5 = (f32[128,6]{0,1:T(8,128)S(1)}, f32[128,6]{0,1:T(8,128)}, u32[]{:S(2)}) copy-start(f32[128,6]{0,1:T(8,128)} %param.11) | copy-start | bytes 9220
  362.3 16.3 %all-to-all-start.1 = ((bf16[4,128,512]{2,1,0:T(8,128)(2,1)}), bf16[4,128,512]{2,1,0:T(8,128)(2,1)S(1)}, u32[]{:S(2)}, u32[]{:S(2)}) async-start(bf16[4,128,512]{2,1,0:T(8,128)(2,1)} %bitcast.96), calls=%async_computation.1 | async-start | bytes 1048576 | tf_op jit(solution)/shard_map/all_to_all | solution.py:41
Sparse Core Ops, SparseCore 0:
  102.7 163.3 all-gather.1
